TPU v7x, 32 devices: a whole 2x2x4 slice. The times are simulated.
32 devices in a mesh: px: 4 (over x, core), py: 8 (over z, y).
Axes of the slice: x: 2, y: 2, z: 4, core: 2. Of those that a mesh axis runs over, the one named last changes fastest.
Arguments:
- metric: bfloat16 [3, 160, 24, 1024], P(None, 'px', None, 'py'), may hold values from 0.25 to 24
- helmholtz: bfloat16 [160, 24, 1024], P('px', None, 'py'), may hold values from 1 to 30
- forcing: bfloat16 [160, 24, 1024], P('px', None, 'py'), may hold values from -6 to 6
- orientation: int32 [160, 1024], P('px', 'py'), may hold values 0 or 1
- start_x: float32 [160, 24, 1024], P('px', None, 'py'), may hold values from -6 to 6
- start_y: float32 [160, 24, 1024], P('px', None, 'py'), may hold values from -6 to 6
- start_z: float32 [160, 25, 1024], P('px', None, 'py'), may hold values from -6 to 6
Outputs:
- trace_x: float32 [160, 24, 1024], P('px', None, 'py')
- trace_y: float32 [160, 24, 1024], P('px', None, 'py')
- trace_z: float32 [160, 25, 1024], P('px', None, 'py')
- pressure: float32 [160, 24, 1024], P('px', None, 'py')
All inputs are finite; a program needn't handle non-finite values. No bound on the sum of `orientation` on one device may be relied on, other than what follows from the above.
Results may differ from a plain program's by a relative error of at most 0.0003.
Values sent between devices are 32-bit elements; how exact they have to be, the bound alone decides.
A program may use at most 64 MiB of HBM per device.

v0:
```python
import jax
import jax.numpy as jnp
from jax import lax
from jax.sharding import PartitionSpec as P

ITERS = 2


def shifted(x, axis, by):
    devices = lax.axis_size(axis)
    return lax.ppermute(x, axis, [(i, (i + by) % devices) for i in range(devices)])


def coefficients(metric, helmholtz, orientation):
    metric_x = metric[0].astype(jnp.float32)
    metric_y = metric[1].astype(jnp.float32)
    metric_z = metric[2].astype(jnp.float32)
    turned = (orientation == 1)[:, None, :]
    inverse_x = 1.0 / jnp.where(turned, metric_y, metric_x)
    inverse_y = 1.0 / jnp.where(turned, metric_x, metric_y)
    inverse_z = 1.0 / metric_z
    denominator = helmholtz.astype(jnp.float32) + 2.0 * (
        3.0 * inverse_x + 3.0 * inverse_y + 3.0 * inverse_z
    )
    return (inverse_x, inverse_y, inverse_z, denominator)


def element(
    trace_west, trace_east, trace_south, trace_north, trace_bottom, trace_top, coeffs, source
):
    inverse_x, inverse_y, inverse_z, denominator = coeffs
    weight_x = 3.0 * inverse_x
    weight_y = 3.0 * inverse_y
    weight_z = 3.0 * inverse_z
    gathered = (
        weight_x * (trace_west + trace_east)
        + weight_y * (trace_south + trace_north)
        + weight_z * (trace_bottom + trace_top)
    )
    pressure = (source + gathered) / denominator
    flux_west = inverse_x * (2.0 * trace_west + trace_east) - weight_x * pressure
    flux_east = inverse_x * (trace_west + 2.0 * trace_east) - weight_x * pressure
    flux_south = inverse_y * (2.0 * trace_south + trace_north) - weight_y * pressure
    flux_north = inverse_y * (trace_south + 2.0 * trace_north) - weight_y * pressure
    flux_bottom = inverse_z * (2.0 * trace_bottom + trace_top) - weight_z * pressure
    flux_top = inverse_z * (trace_bottom + 2.0 * trace_top) - weight_z * pressure
    return (flux_west, flux_east, flux_south, flux_north, flux_bottom, flux_top, pressure)


def stack_vertical(flux_bottom, flux_top):
    zero_layer = jnp.zeros_like(flux_bottom[:, :1])
    return jnp.concatenate([flux_bottom, zero_layer], 1) + jnp.concatenate(
        [zero_layer, flux_top], 1
    )


def neighbours(field_x, field_y):
    from_east = shifted(field_x[:1], "px", -1)
    from_north = shifted(field_y[:, :, :1], "py", -1)
    east_side = jnp.concatenate([field_x[1:], from_east], 0)
    north_side = jnp.concatenate([field_y[:, :, 1:], from_north], 2)
    return (east_side, north_side)


def owned_apply(fields, coeffs, source):
    field_x, field_y, field_z = fields
    east_side, north_side = neighbours(field_x, field_y)
    fluxes = element(
        field_x, east_side, field_y, north_side, field_z[:, :-1], field_z[:, 1:], coeffs, source
    )
    from_west = shifted(fluxes[1][-1:], "px", 1)
    from_south = shifted(fluxes[3][:, :, -1:], "py", 1)
    sum_x = fluxes[0] + jnp.concatenate([from_west, fluxes[1][:-1]], 0)
    sum_y = fluxes[2] + jnp.concatenate([from_south, fluxes[3][:, :, :-1]], 2)
    return (sum_x, sum_y, stack_vertical(fluxes[4], fluxes[5]))


def owned_pressure(fields, coeffs, source):
    field_x, field_y, field_z = fields
    east_side, north_side = neighbours(field_x, field_y)
    return element(
        field_x, east_side, field_y, north_side, field_z[:, :-1], field_z[:, 1:], coeffs, source
    )[6]


def owned_inner(first_vec, second_vec):
    return (
        jnp.sum(first_vec[0] * second_vec[0])
        + jnp.sum(first_vec[1] * second_vec[1])
        + jnp.sum(first_vec[2] * second_vec[2])
    )


def combine(first_vec, scale, second_vec):
    return tuple((member + scale * other for member, other in zip(first_vec, second_vec)))


def pair_sums(norm_part, curve_part):
    return lax.psum((norm_part, curve_part), ("px", "py"))


def local(metric, helmholtz, forcing, orientation, start_x, start_y, start_z):
    coeffs = coefficients(metric, helmholtz, orientation)
    source = forcing.astype(jnp.float32)
    traces = (start_x, start_y, start_z)
    sums = owned_apply(traces, coeffs, source)
    residual = tuple((-member for member in sums))
    applied = owned_apply(residual, coeffs, 0.0)
    norm_now, curvature_sum = pair_sums(
        owned_inner(residual, residual), owned_inner(residual, applied)
    )
    step_size = norm_now / curvature_sum
    direction = residual
    image_dir = applied
    for iteration in range(ITERS):
        traces = combine(traces, step_size, direction)
        residual = combine(residual, -step_size, image_dir)
        if iteration + 1 < ITERS:
            applied = owned_apply(residual, coeffs, 0.0)
            norm_next, curvature_sum = pair_sums(
                owned_inner(residual, residual), owned_inner(residual, applied)
            )
            beta_ratio = norm_next / norm_now
            step_size = norm_next / (curvature_sum - beta_ratio * norm_next / step_size)
            direction = combine(residual, beta_ratio, direction)
            image_dir = combine(applied, beta_ratio, image_dir)
            norm_now = norm_next
    pressure = owned_pressure(traces, coeffs, source)
    return (traces[0], traces[1], traces[2], pressure)


def solution(mesh):
    return jax.shard_map(
        local,
        mesh=mesh,
        in_specs=(
            P(None, "px", None, "py"),
            P("px", None, "py"),
            P("px", None, "py"),
            P("px", "py"),
            P("px", None, "py"),
            P("px", None, "py"),
            P("px", None, "py"),
        ),
        out_specs=(
            P("px", None, "py"),
            P("px", None, "py"),
            P("px", None, "py"),
            P("px", None, "py"),
        ),
        check_vma=False,
    )
```

profile of v0, /device:TPU:0, one launch (start us, length us, event | category | flops | bytes accessed | tf_op | source)
XLA Modules:
  0.0 218.1 jit_solution(1400882050048215118)
XLA Ops:
  0.6 0.7 slice.120
  1.4 2.4 %collective-permute-start = (f32[1,24,128]{2,1,0:T(8,128)S(1)}, f32[1,24,128]{2,1,0:T(8,128)S(1)}, u32[]{:S(2)}, u32[]{:S(2)}) collective-permute-start(f32[1,24,128]{2,1,0:T(8,128)S(1)} %slice.120), channel_id=1, source_target_pairs={{0,24},{8,0},{16,8},{24,16},{1,25},{9,1},{17,9},{25,17},{2,26},{10... | collective-permute-start | bytes 36872 | tf_op jit(solution)/shard_map/ppermute | solution.py:11
  3.8 4.6 %collective-permute-start.1 = (f32[40,24,1]{2,1,0:T(8,128)}, f32[40,24,1]{2,1,0:T(8,128)S(1)}, u32[]{:S(2)}, u32[]{:S(2)}) collective-permute-start(f32[40,24,1]{2,1,0:T(8,128)} %bitcast.161), channel_id=1, source_target_pairs={{0,7},{1,0},{2,1},{3,2},{4,3},{5,4},{6,5},{7,6},{8,15},{9,8},{10,9... | collective-permute-start | bytes 11528 | tf_op jit(solution)/shard_map/ppermute | solution.py:11
  8.3 1.1 slice.119
  9.5 0.2 slice.121
  9.8 9.0 %collective-permute-done.1 = f32[40,24,1]{2,1,0:T(8,128)S(1)} collective-permute-done((f32[40,24,1]{2,1,0:T(8,128)}, f32[40,24,1]{2,1,0:T(8,128)S(1)}, u32[]{:S(2)}, u32[]{:S(2)}) %collective-permute-start.1) | collective-permute-done | bytes 3872 | tf_op jit(solution)/shard_map/ppermute | solution.py:11
  18.9 0.7 multiply_subtract_fusion.4
  19.6 0.2 slice.160
  19.8 0.3 collective-permute-start.3
  20.1 14.9 %collective-permute-done.3 = f32[40,24,1]{2,1,0:T(8,128)S(1)} collective-permute-done((f32[40,24,1]{2,1,0:T(8,128)S(1)}, f32[40,24,1]{2,1,0:T(8,128)S(1)}, u32[]{:S(2)}, u32[]{:S(2)}) %collective-permute-start.3) | collective-permute-done | bytes 3872 | tf_op jit(solution)/shard_map/ppermute | solution.py:11
  35.1 0.6 fusion.23
  35.7 0.2 slice.164
  35.9 1.8 collective-permute-start.5
  37.7 1.1 collective-permute-done.2
  38.8 0.5 fusion.13
  39.3 0.4 collective-permute-start.4
  39.7 0.8 multiply_reduce_fusion.3
  40.6 8.0 %collective-permute-done.5 = f32[40,24,1]{2,1,0:T(8,128)S(1)} collective-permute-done((f32[40,24,1]{2,1,0:T(8,128)S(1)}, f32[40,24,1]{2,1,0:T(8,128)S(1)}, u32[]{:S(2)}, u32[]{:S(2)}) %collective-permute-start.5) | collective-permute-done | bytes 3872 | tf_op jit(solution)/shard_map/ppermute | solution.py:11
  48.5 0.7 fusion.15
  49.3 0.5 fusion.16
  49.8 0.2 slice.170
  50.0 16.4 %collective-permute-done.7 = f32[40,24,1]{2,1,0:T(8,128)S(1)} collective-permute-done((f32[40,24,1]{2,1,0:T(8,128)S(1)}, f32[40,24,1]{2,1,0:T(8,128)S(1)}, u32[]{:S(2)}, u32[]{:S(2)}) %collective-permute-start.7) | collective-permute-done | bytes 3872 | tf_op jit(solution)/shard_map/ppermute | solution.py:11
  66.4 1.3 multiply_reduce_fusion.6
  67.7 0.2 collective-permute-start.6
  68.0 0.8 multiply_reduce_fusion.2
  68.8 2.0 collective-permute-done.6
  70.9 1.0 multiply_reduce_fusion.7
  75.4 36.9 %all-reduce.7 = (f32[]{:T(128)}, f32[]{:T(128)}) all-reduce(f32[]{:T(128)S(6)} %add.255, f32[]{:T(128)S(6)} %add.271), channel_id=1, replica_groups=mesh['px'=4,'py'=8] {'px','py'}, use_global_device_ids=true, to_apply=%region_3.4 | all-reduce | flops 2 | bytes 16 | tf_op jit(solution)/shard_map/psum | solution.py:99
  113.7 0.9 copy-done.5
  114.8 0.3 multiply_add_fusion.5
  115.1 0.6 collective-permute-start.8
  115.7 3.6 %collective-permute-start.9 = (f32[40,24,1]{2,1,0:T(8,128)S(1)}, f32[40,24,1]{2,1,0:T(8,128)S(1)}, u32[]{:S(2)}, u32[]{:S(2)}) collective-permute-start(f32[40,24,1]{2,1,0:T(8,128)S(1)} %bitcast.160), channel_id=1, source_target_pairs={{0,7},{1,0},{2,1},{3,2},{4,3},{5,4},{6,5},{7,6},{8,15},{9,8},{10,9... | collective-permute-start | bytes 11528 | tf_op jit(solution)/shard_map/ppermute | solution.py:11
  119.7 10.7 %collective-permute-done.9 = f32[40,24,1]{2,1,0:T(8,128)S(1)} collective-permute-done((f32[40,24,1]{2,1,0:T(8,128)S(1)}, f32[40,24,1]{2,1,0:T(8,128)S(1)}, u32[]{:S(2)}, u32[]{:S(2)}) %collective-permute-start.9) | collective-permute-done | bytes 3872 | tf_op jit(solution)/shard_map/ppermute | solution.py:11
  130.4 1.5 fusion.17
  131.9 0.4 multiply_subtract_fusion.1
  132.6 1.7 collective-permute-start.11
  134.4 15.1 %collective-permute-done.11 = f32[40,24,1]{2,1,0:T(8,128)S(1)} collective-permute-done((f32[40,24,1]{2,1,0:T(8,128)S(1)}, f32[40,24,1]{2,1,0:T(8,128)S(1)}, u32[]{:S(2)}, u32[]{:S(2)}) %collective-permute-start.11) | collective-permute-done | bytes 3872 | tf_op jit(solution)/shard_map/ppermute | solution.py:11
  149.5 2.3 %fusion.9 = (f32[]{:T(128)}, f32[]{:T(128)}, f32[]{:T(128)}, f32[]{:T(128)}, f32[40,24,128]{2,1,0:T(8,128)}) fusion(f32[40,24,128]{2,1,0:T(8,128)S(1)} %multiply_add_fusion.4, f32[40,24,127]{2,1,0:T(8,128)S(1)} %bitcast.164, f32[40,24,1]{2,1,0:T(8,128)S(1)} %collective-permute-done.11, f32[40,24,128]{2,1,0:T(8,128)S(1)} %get-tuple-element.23, ...), kind=kLoop, calls=%fused_computation.34 | loop fusion | flops 4915196 | bytes 5657616 | tf_op jit(solution)/shard_map/reduce_sum | solution.py:89
  154.3 2.0 multiply_reduce_fusion
  157.6 38.2 %all-reduce.6 = (f32[]{:T(128)}, f32[]{:T(128)}) all-reduce(f32[]{:T(128)S(6)} %add.277, f32[]{:T(128)S(6)} %add.293), channel_id=1, replica_groups=mesh['px'=4,'py'=8] {'px','py'}, use_global_device_ids=true, to_apply=%region_11.12 | all-reduce | flops 2 | bytes 16 | tf_op jit(solution)/shard_map/psum | solution.py:99
  200.4 1.4 multiply_add_fusion.2
  201.9 0.9 collective-permute-start.12
  202.8 2.7 %collective-permute-start.13 = (f32[40,24,1]{2,1,0:T(8,128)S(1)}, f32[40,24,1]{2,1,0:T(8,128)S(1)}, u32[]{:S(2)}, u32[]{:S(2)}) collective-permute-start(f32[40,24,1]{2,1,0:T(8,128)S(1)} %bitcast.163), channel_id=1, source_target_pairs={{0,7},{1,0},{2,1},{3,2},{4,3},{5,4},{6,5},{7,6},{8,15},{9,8},{10,9... | collective-permute-start | bytes 11528 | tf_op jit(solution)/shard_map/ppermute | solution.py:11
  205.5 0.2 multiply_add_fusion
  205.8 0.2 slice.184
  206.0 1.1 copy.14
  207.1 9.5 %collective-permute-done.13 = f32[40,24,1]{2,1,0:T(8,128)S(1)} collective-permute-done((f32[40,24,1]{2,1,0:T(8,128)S(1)}, f32[40,24,1]{2,1,0:T(8,128)S(1)}, u32[]{:S(2)}, u32[]{:S(2)}) %collective-permute-start.13) | collective-permute-done | bytes 3872 | tf_op jit(solution)/shard_map/ppermute | solution.py:11
  216.6 1.4 fusion.1
  (75 shorter events, 1.5 us)
Async XLA Ops:
  0.6 7.7 %copy-start.23 = (s32[40,128]{1,0:T(8,128)S(1)}, s32[40,128]{1,0:T(8,128)}, u32[]{:S(2)}) copy-start(s32[40,128]{1,0:T(8,128)} %param.10) | copy-start | bytes 61444
  1.4 17.5 %collective-permute-start = (f32[1,24,128]{2,1,0:T(8,128)S(1)}, f32[1,24,128]{2,1,0:T(8,128)S(1)}, u32[]{:S(2)}, u32[]{:S(2)}) collective-permute-start(f32[1,24,128]{2,1,0:T(8,128)S(1)} %slice.120), channel_id=1, source_target_pairs={{0,24},{8,0},{16,8},{24,16},{1,25},{9,1},{17,9},{25,17},{2,26},{10... | collective-permute-start | bytes 36872 | tf_op jit(solution)/shard_map/ppermute | solution.py:11
  3.8 5.7 %copy-start.6 = (f32[40,24,128]{2,1,0:T(8,128)S(1)}, f32[40,24,128]{2,1,0:T(8,128)}, u32[]{:S(2)}) copy-start(f32[40,24,128]{2,1,0:T(8,128)} %param.12) | copy-start | bytes 1474564
  3.8 15.1 %collective-permute-start.1 = (f32[40,24,1]{2,1,0:T(8,128)}, f32[40,24,1]{2,1,0:T(8,128)S(1)}, u32[]{:S(2)}, u32[]{:S(2)}) collective-permute-start(f32[40,24,1]{2,1,0:T(8,128)} %bitcast.161), channel_id=1, source_target_pairs={{0,7},{1,0},{2,1},{3,2},{4,3},{5,4},{6,5},{7,6},{8,15},{9,8},{10,9... | collective-permute-start | bytes 11528 | tf_op jit(solution)/shard_map/ppermute | solution.py:11
  8.3 1.4 copy-start.19
  9.5 9.4 %copy-start.2 = (f32[40,24,128]{2,1,0:T(8,128)S(1)}, f32[40,24,128]{2,1,0:T(8,128)}, u32[]{:S(2)}) copy-start(f32[40,24,128]{2,1,0:T(8,128)} %param.11) | copy-start | bytes 1474564
  9.5 9.4 %copy-start.21 = (bf16[40,24,128]{2,1,0:T(8,128)(2,1)S(1)}, bf16[40,24,128]{2,1,0:T(8,128)(2,1)}, u32[]{:S(2)}) copy-start(bf16[40,24,128]{2,1,0:T(8,128)(2,1)} %param.9) | copy-start | bytes 737284
  9.7 9.2 %copy-start = (bf16[3,40,24,128]{3,2,1,0:T(8,128)(2,1)S(1)}, bf16[3,40,24,128]{3,2,1,0:T(8,128)(2,1)}, u32[]{:S(2)}) copy-start(bf16[3,40,24,128]{3,2,1,0:T(8,128)(2,1)} %param.7) | copy-start | bytes 2211844
  9.7 9.2 %copy-start.16 = (bf16[40,24,128]{2,1,0:T(8,128)(2,1)S(1)}, bf16[40,24,128]{2,1,0:T(8,128)(2,1)}, u32[]{:S(2)}) copy-start(bf16[40,24,128]{2,1,0:T(8,128)(2,1)} %param.8) | copy-start | bytes 737284
  19.8 15.2 %collective-permute-start.3 = (f32[40,24,1]{2,1,0:T(8,128)S(1)}, f32[40,24,1]{2,1,0:T(8,128)S(1)}, u32[]{:S(2)}, u32[]{:S(2)}) collective-permute-start(f32[40,24,1]{2,1,0:T(8,128)S(1)} %slice.160), channel_id=1, source_target_pairs={{0,1},{1,2},{2,3},{3,4},{4,5},{5,6},{6,7},{7,0},{8,9},{9,10},{10,1... | collective-permute-start | bytes 11528 | tf_op jit(solution)/shard_map/ppermute | solution.py:11
  35.6 3.2 %collective-permute-start.2 = (f32[1,24,128]{2,1,0:T(8,128)S(1)}, f32[1,24,128]{2,1,0:T(8,128)S(1)}, u32[]{:S(2)}, u32[]{:S(2)}) collective-permute-start(f32[1,24,128]{2,1,0:T(8,128)S(1)} %slice.158), channel_id=1, source_target_pairs={{0,8},{8,16},{16,24},{24,0},{1,9},{9,17},{17,25},{25,1},{2,10},{10... | collective-permute-start | bytes 36872 | tf_op jit(solution)/shard_map/ppermute | solution.py:11
  35.9 12.6 %collective-permute-start.5 = (f32[40,24,1]{2,1,0:T(8,128)S(1)}, f32[40,24,1]{2,1,0:T(8,128)S(1)}, u32[]{:S(2)}, u32[]{:S(2)}) collective-permute-start(f32[40,24,1]{2,1,0:T(8,128)S(1)} %bitcast.166), channel_id=1, source_target_pairs={{0,7},{1,0},{2,1},{3,2},{4,3},{5,4},{6,5},{7,6},{8,15},{9,8},{10,9... | collective-permute-start | bytes 11528 | tf_op jit(solution)/shard_map/ppermute | solution.py:11
  39.3 9.2 %collective-permute-start.4 = (f32[1,24,128]{2,1,0:T(8,128)S(1)}, f32[1,24,128]{2,1,0:T(8,128)S(1)}, u32[]{:S(2)}, u32[]{:S(2)}) collective-permute-start(f32[1,24,128]{2,1,0:T(8,128)S(1)} %slice.163), channel_id=1, source_target_pairs={{0,24},{8,0},{16,8},{24,16},{1,25},{9,1},{17,9},{25,17},{2,26},{10... | collective-permute-start | bytes 36872 | tf_op jit(solution)/shard_map/ppermute | solution.py:11
  40.6 30.3 %copy-start.4 = (f32[39,24,128]{2,1,0:T(8,128)}, f32[39,24,128]{2,1,0:T(8,128)S(1)}, u32[]{:S(2)}) copy-start(f32[39,24,128]{2,1,0:T(8,128)S(1)} %slice.162) | copy-start | bytes 1437700
  49.3 18.7 %copy-start.7 = (f32[40,24,128]{2,1,0:T(8,128)}, f32[40,24,128]{2,1,0:T(8,128)S(1)}, u32[]{:S(2)}) copy-start(f32[40,24,128]{2,1,0:T(8,128)S(1)} %get-tuple-element.24) | copy-start | bytes 1474564
  49.8 18.2 %copy-start.9 = (f32[40,24,128]{2,1,0:T(8,128)}, f32[40,24,128]{2,1,0:T(8,128)S(1)}, u32[]{:S(2)}) copy-start(f32[40,24,128]{2,1,0:T(8,128)S(1)} %get-tuple-element.40) | copy-start | bytes 1474564
  50.0 16.4 %collective-permute-start.7 = (f32[40,24,1]{2,1,0:T(8,128)S(1)}, f32[40,24,1]{2,1,0:T(8,128)S(1)}, u32[]{:S(2)}, u32[]{:S(2)}) collective-permute-start(f32[40,24,1]{2,1,0:T(8,128)S(1)} %slice.170), channel_id=1, source_target_pairs={{0,1},{1,2},{2,3},{3,4},{4,5},{5,6},{6,7},{7,0},{8,9},{9,10},{10,1... | collective-permute-start | bytes 11528 | tf_op jit(solution)/shard_map/ppermute | solution.py:11
  67.7 3.1 %collective-permute-start.6 = (f32[1,24,128]{2,1,0:T(8,128)S(1)}, f32[1,24,128]{2,1,0:T(8,128)S(1)}, u32[]{:S(2)}, u32[]{:S(2)}) collective-permute-start(f32[1,24,128]{2,1,0:T(8,128)S(1)} %slice.168), channel_id=1, source_target_pairs={{0,8},{8,16},{16,24},{24,0},{1,9},{9,17},{17,25},{25,1},{2,10},{10... | collective-permute-start | bytes 36872 | tf_op jit(solution)/shard_map/ppermute | solution.py:11
  68.8 3.0 %copy-start.14 = (f32[39,24,128]{2,1,0:T(8,128)}, f32[39,24,128]{2,1,0:T(8,128)S(1)}, u32[]{:S(2)}) copy-start(f32[39,24,128]{2,1,0:T(8,128)S(1)} %slice.169) | copy-start | bytes 1437700
  113.6 1.0 copy-start.5
  113.6 1.2 copy-start.15
  114.8 34.7 %copy-start.1 = (f32[40,24,128]{2,1,0:T(8,128)}, f32[40,24,128]{2,1,0:T(8,128)S(1)}, u32[]{:S(2)}) copy-start(f32[40,24,128]{2,1,0:T(8,128)S(1)} %multiply_add_fusion.4) | copy-start | bytes 1474564
  114.8 4.6 %copy-start.8 = (f32[40,24,128]{2,1,0:T(8,128)S(1)}, f32[40,24,128]{2,1,0:T(8,128)}, u32[]{:S(2)}) copy-start(f32[40,24,128]{2,1,0:T(8,128)} %copy-done.7) | copy-start | bytes 1474564
  114.8 4.6 %copy-start.10 = (f32[40,24,128]{2,1,0:T(8,128)S(1)}, f32[40,24,128]{2,1,0:T(8,128)}, u32[]{:S(2)}) copy-start(f32[40,24,128]{2,1,0:T(8,128)} %copy-done.9) | copy-start | bytes 1474564
  115.1 15.4 %collective-permute-start.8 = (f32[1,24,128]{2,1,0:T(8,128)S(1)}, f32[1,24,128]{2,1,0:T(8,128)S(1)}, u32[]{:S(2)}, u32[]{:S(2)}) collective-permute-start(f32[1,24,128]{2,1,0:T(8,128)S(1)} %slice.173), channel_id=1, source_target_pairs={{0,24},{8,0},{16,8},{24,16},{1,25},{9,1},{17,9},{25,17},{2,26},{10... | collective-permute-start | bytes 36872 | tf_op jit(solution)/shard_map/ppermute | solution.py:11
  115.7 14.7 %collective-permute-start.9 = (f32[40,24,1]{2,1,0:T(8,128)S(1)}, f32[40,24,1]{2,1,0:T(8,128)S(1)}, u32[]{:S(2)}, u32[]{:S(2)}) collective-permute-start(f32[40,24,1]{2,1,0:T(8,128)S(1)} %bitcast.160), channel_id=1, source_target_pairs={{0,7},{1,0},{2,1},{3,2},{4,3},{5,4},{6,5},{7,6},{8,15},{9,8},{10,9... | collective-permute-start | bytes 11528 | tf_op jit(solution)/shard_map/ppermute | solution.py:11
  119.5 10.9 %copy-start.17 = (bf16[40,24,128]{2,1,0:T(8,128)(2,1)S(1)}, bf16[40,24,128]{2,1,0:T(8,128)(2,1)}, u32[]{:S(2)}) copy-start(bf16[40,24,128]{2,1,0:T(8,128)(2,1)} %param.8) | copy-start | bytes 737284
  132.3 17.2 %collective-permute-start.10 = (f32[1,24,128]{2,1,0:T(8,128)S(1)}, f32[1,24,128]{2,1,0:T(8,128)S(1)}, u32[]{:S(2)}, u32[]{:S(2)}) collective-permute-start(f32[1,24,128]{2,1,0:T(8,128)S(1)} %slice.178), channel_id=1, source_target_pairs={{0,8},{8,16},{16,24},{24,0},{1,9},{9,17},{17,25},{25,1},{2,10},{10... | collective-permute-start | bytes 36872 | tf_op jit(solution)/shard_map/ppermute | solution.py:11
  132.6 16.9 %collective-permute-start.11 = (f32[40,24,1]{2,1,0:T(8,128)S(1)}, f32[40,24,1]{2,1,0:T(8,128)S(1)}, u32[]{:S(2)}, u32[]{:S(2)}) collective-permute-start(f32[40,24,1]{2,1,0:T(8,128)S(1)} %slice.180), channel_id=1, source_target_pairs={{0,1},{1,2},{2,3},{3,4},{4,5},{5,6},{6,7},{7,0},{8,9},{9,10},{10,1... | collective-permute-start | bytes 11528 | tf_op jit(solution)/shard_map/ppermute | solution.py:11
  200.3 1.4 copy-start.3
  201.7 14.9 %copy-start.11 = (f32[40,24,128]{2,1,0:T(8,128)}, f32[40,24,128]{2,1,0:T(8,128)S(1)}, u32[]{:S(2)}) copy-start(f32[40,24,128]{2,1,0:T(8,128)S(1)} %multiply_add_fusion.2) | copy-start | bytes 1474564
  201.7 3.8 %copy-start.20 = (f32[40,25,128]{2,0,1:T(8,128)S(1)}, f32[40,25,128]{2,0,1:T(8,128)}, u32[]{:S(2)}) copy-start(f32[40,25,128]{2,0,1:T(8,128)} %param.13) | copy-start | bytes 1536004
  201.9 3.9 %copy-start.12 = (f32[40,24,128]{2,1,0:T(8,128)}, f32[40,24,128]{2,1,0:T(8,128)S(1)}, u32[]{:S(2)}) copy-start(f32[40,24,128]{2,1,0:T(8,128)S(1)} %multiply_add_fusion.3) | copy-start | bytes 1474564
  201.9 14.7 %collective-permute-start.12 = (f32[1,24,128]{2,1,0:T(8,128)S(1)}, f32[1,24,128]{2,1,0:T(8,128)S(1)}, u32[]{:S(2)}, u32[]{:S(2)}) collective-permute-start(f32[1,24,128]{2,1,0:T(8,128)S(1)} %slice.183), channel_id=1, source_target_pairs={{0,24},{8,0},{16,8},{24,16},{1,25},{9,1},{17,9},{25,17},{2,26},{10... | collective-permute-start | bytes 36872 | tf_op jit(solution)/shard_map/ppermute | solution.py:11
  202.8 13.8 %collective-permute-start.13 = (f32[40,24,1]{2,1,0:T(8,128)S(1)}, f32[40,24,1]{2,1,0:T(8,128)S(1)}, u32[]{:S(2)}, u32[]{:S(2)}) collective-permute-start(f32[40,24,1]{2,1,0:T(8,128)S(1)} %bitcast.163), channel_id=1, source_target_pairs={{0,7},{1,0},{2,1},{3,2},{4,3},{5,4},{6,5},{7,6},{8,15},{9,8},{10,9... | collective-permute-start | bytes 11528 | tf_op jit(solution)/shard_map/ppermute | solution.py:11
  205.7 10.9 %copy-start.18 = (bf16[40,24,128]{2,1,0:T(8,128)(2,1)S(1)}, bf16[40,24,128]{2,1,0:T(8,128)(2,1)}, u32[]{:S(2)}) copy-start(bf16[40,24,128]{2,1,0:T(8,128)(2,1)} %param.8) | copy-start | bytes 737284
  205.7 10.8 %copy-start.22 = (bf16[40,24,128]{2,1,0:T(8,128)(2,1)S(1)}, bf16[40,24,128]{2,1,0:T(8,128)(2,1)}, u32[]{:S(2)}) copy-start(bf16[40,24,128]{2,1,0:T(8,128)(2,1)} %param.9) | copy-start | bytes 737284
  206.0 10.7 %copy-start.13 = (f32[40,24,128]{2,1,0:T(8,128)S(1)}, f32[40,24,128]{2,1,0:T(8,128)}, u32[]{:S(2)}) copy-start(f32[40,24,128]{2,1,0:T(8,128)} %copy-done.12) | copy-start | bytes 1474564
  206.0 10.7 %slice-start = ((f32[40,24,128]{2,1,0:T(8,128)}), f32[39,24,128]{2,1,0:T(8,128)S(1)}, s32[]{:S(2)}) async-start(f32[40,24,128]{2,1,0:T(8,128)} %copy-done.12), calls=%async_computation | async-start | bytes 958464 | tf_op jit(solution)/shard_map/slice | solution.py:60
where the time goes:
time: 219 us; the launch traced here: 218 us
  waiting for transfers between devices  86.8 us (40%)
  blocking collectives  75.1 us (34%)
  starting transfers between devices  19.5 us (9%)
  other arithmetic  16.7 us (8%)
  between operations  14.2 us (6%)
  local copies, waits for them, and re-layouts  5.79 us (3%)
    ppermute x14, waiting for transfers between devices, shifted(): lax.ppermute(x, axis, [(i, (i + by) % devices) for i in range(devices)])  86.8 us
    psum x2, blocking collectives, pair_sums(): return lax.psum((norm_part, curve_part), ('px', 'py'))  75.1 us
    ppermute x14, starting transfers between devices, shifted(): lax.ppermute(x, axis, [(i, (i + by) % devices) for i in range(devices)])  19.5 us
  transfers between devices with their start and end apart: 14, of which 9 were waited for; matrix products, arithmetic and copies ran while one was open for 3% of the time, Pallas kernels for 0%

commit v1 on v0

v1 whole, which is shorter than its diff:
```python
import functools

import jax
import jax.numpy as jnp
from jax import lax
from jax.experimental import pallas as pl
from jax.experimental.pallas import tpu as pltpu
from jax.sharding import PartitionSpec as P

MESH = pl.DeviceIdType.MESH
F32 = jnp.float32


def fold(x):
    total = x[0:8]
    for row in range(8, x.shape[0], 8):
        total = total + x[row : row + 8]
    return total


def kernel(
    npx, npy,
    met_h, hel_h, src_h, ori_h, sx_h, sy_h, sz_h,
    ox, oy, oz, op,
    met, hel, src, ori, xs, ys, zs,
    ix, iy, iz, di, p0, p1, p2, rx, ry, rz, vx, vy, vz,
    strip, nsend1, esend1, nsend2, esend2,
    hy, cx, cy, nrecv1, erecv1, nrecv2, erecv2,
    mom, slots1, slots2,
    in_sem, send_sem, recv_sem,
):
    nx, levels, ny = hel.shape
    unroll = next(u for u in (8, 5, 4, 2, 1) if nx % u == 0)
    px, py = lax.axis_index("px"), lax.axis_index("py")

    def device(dx, dy):
        return (lax.rem(px + dx + npx, npx), lax.rem(py + dy + npy, npy))

    loads = []
    for n, (a, b) in enumerate(
        (
            (sx_h, xs.at[pl.ds(0, nx)]), (sy_h, ys), (met_h, met), (ori_h, ori),
            (hel_h, hel), (src_h, src), (sz_h, zs),
        )
    ):
        copy = pltpu.make_async_copy(a, b, in_sem.at[n])
        copy.start()
        loads.append(copy)

    offsets = {(1, 0), (-1, 0), (0, 1), (0, -1), (-1, 1), (1, -1)}
    offsets |= {(d, 0) for d in range(1, npx)} | {(0, d) for d in range(1, npy)}
    offsets = sorted({(a % npx, b % npy) for a, b in offsets} - {(0, 0)})
    barrier = pltpu.get_barrier_semaphore()
    for a, b in offsets:
        pl.semaphore_signal(barrier, inc=1, device_id=device(a, b), device_id_type=MESH)
    pl.semaphore_wait(barrier, len(offsets))

    count = [0]
    sent = []

    def send(source, target, dx, dy):
        n = count[0]
        count[0] += 1
        copy = pltpu.make_async_remote_copy(
            src_ref=source, dst_ref=target, send_sem=send_sem.at[n], recv_sem=recv_sem.at[n],
            device_id=device(dx, dy), device_id_type=MESH,
        )
        copy.start()
        sent.append(copy)
        return copy

    lane = lax.broadcasted_iota(jnp.int32, (levels, ny), 1)
    first, last = lane == 0, lane == ny - 1
    zero = jnp.zeros((levels, ny), F32)
    zero8 = jnp.zeros((8, ny), F32)

    def loop(body, carry):
        def block(b, carry):
            for u in range(unroll):
                carry = body(b * unroll + u, carry)
            return carry

        return lax.fori_loop(0, nx // unroll, block, carry)

    def pack_first(i, y, held):
        return jnp.where(lane == i, pltpu.roll(y, i, 1), held)

    def pack_last(i, y, held):
        return jnp.where(lane == i, pltpu.roll(y, i + 1, 1), held)

    def partial(i, xf, yf, zf, a, b, c, d, source):
        w = xf[i]
        e = jnp.where(i < nx - 1, xf[jnp.minimum(i + 1, nx - 1)], 0.0)
        s = yf[i]
        n = jnp.where(last, 0.0, pltpu.roll(s, ny - 1, 1))
        bottom, top = zf[i, pl.ds(0, levels), :], zf[i, pl.ds(1, levels), :]
        total = 3.0 * (a * (w + e) + b * (s + n) + c * (bottom + top))
        if source is not None:
            total = total + source
        return total * d

    def complete(phase, xf, yf, zf, pf, coming, nb, eb, nco, eco):
        for copy in coming:
            copy.wait_recv()
        end = nx - 1
        pf[end] = pf[end] + 3.0 * ix[end] * di[end] * xf[nx]
        mine = strip[phase]
        iyh, kh = nco[2], nco[3]
        north_p = nb[1] + kh * mine + jnp.where(
            lane == end, pltpu.roll(kh, ny - 1, 1) * pltpu.roll(cx[phase], nx, 1), 0.0
        )
        flux_strip = iyh * (2.0 * mine + nb[0] - 3.0 * north_p)
        e = xf[0]
        west_p = eb[1] + eco[3] * e + jnp.where(
            last, eco[4] * pltpu.roll(cy[phase], ny - nx, 1), 0.0
        )
        flux_west_halo = eco[2] * (2.0 * e + eb[0] - 3.0 * west_p)
        north_strip = hy[phase]

        def column(i, flux_east):
            w, e, s = xf[i], xf[i + 1], yf[i]
            bottom, top = zf[i, pl.ds(0, levels), :], zf[i, pl.ds(1, levels), :]
            a, b, c = ix[i], iy[i], iz[i]
            halo = pltpu.roll(north_strip, ny - 1 - i, 1)
            n = jnp.where(last, halo, pltpu.roll(s, ny - 1, 1))
            p = pf[i] + jnp.where(last, 3.0 * b * di[i] * halo, 0.0)
            pf[i] = p
            sumx, sumy, sumz = w + e - 3.0 * p, s + n - 3.0 * p, bottom + top - 3.0 * p
            fx = a * (w + sumx) + flux_east
            flux_east = a * (e + sumx)
            north = pltpu.roll(b * (n + sumy), 1, 1)
            fy = b * (s + sumy) + jnp.where(
                first, pltpu.roll(flux_strip, lax.rem(ny - i, ny), 1), north
            )
            fz = jnp.concatenate([c * (bottom + sumz), zero8], 0) + pltpu.roll(
                jnp.concatenate([c * (top + sumz), zero8], 0), 1, 0
            )
            return fx, fy, fz, flux_east

        return column, flux_west_halo

    loads[0].wait()
    coming = [send(xs.at[0], xs.at[nx], -1, 0), send(xs.at[0], cx.at[0], -1, 1)]
    for copy in loads[1:]:
        copy.wait()

    def body(i, held):
        h0, s1, q1, b1, k1 = held
        turned = ori[pl.ds(i, 1), :] == 1
        mx, my, mz = met[0, i].astype(F32), met[1, i].astype(F32), met[2, i].astype(F32)
        a = 1.0 / jnp.where(turned, my, mx)
        b = 1.0 / jnp.where(turned, mx, my)
        c = 1.0 / mz
        d = 1.0 / (hel[i].astype(F32) + 6.0 * (a + b + c))
        ix[i], iy[i], iz[i], di[i] = a, b, c, d
        p = partial(i, xs, ys, zs, a, b, c, d, src[i].astype(F32))
        p0[i] = p
        s = ys[i]
        return (
            pack_first(i, s, h0), pack_last(i, s, s1), pack_last(i, p, q1),
            pack_last(i, b, b1), pack_last(i, 3.0 * b * d, k1),
        )

    h0, s1, q1, b1, k1 = loop(body, (zero,) * 5)
    end = nx - 1
    kx_end = 3.0 * ix[end] * di[end]
    strip[0] = h0
    nsend1[0], nsend1[1], nsend1[2] = s1, q1, b1
    nsend1[3] = pack_last(nx, kx_end, k1)
    esend1[0], esend1[1], esend1[2] = xs[end], p0[end], ix[end]
    esend1[3], esend1[4] = kx_end, 3.0 * iy[end] * di[end]
    coming += [
        send(esend1, erecv1, 1, 0), send(nsend1, nrecv1, 0, 1),
        send(strip.at[0], hy.at[0], 0, -1), send(strip.at[0], cy.at[0], 1, -1),
    ]

    column, flux = complete(0, xs, ys, zs, p0, coming, nrecv1, erecv1, nrecv1, erecv1)

    def body(i, held):
        flux, h0, s1, m0 = held
        fx, fy, fz, flux = column(i, flux)
        fx, fy, fz = -fx, -fy, -fz
        rx[i], ry[i], rz[i] = fx, fy, fz
        m0 = m0 + fold(fx * fx + fy * fy) + fold(fz * fz)
        return flux, pack_first(i, fy, h0), pack_last(i, fy, s1), m0

    flux, h0, s1, m0 = loop(body, (flux, zero, zero, zero8))
    strip[1] = h0
    nsend2[0] = s1
    esend2[0] = rx[end]
    coming = [
        send(rx.at[0], rx.at[nx], -1, 0), send(rx.at[0], cx.at[1], -1, 1),
        send(strip.at[1], hy.at[1], 0, -1), send(strip.at[1], cy.at[1], 1, -1),
    ]

    def body(i, q1):
        p = partial(i, rx, ry, rz, ix[i], iy[i], iz[i], di[i], None)
        p1[i] = p
        return pack_last(i, p, q1)

    q1 = loop(body, zero)
    nsend2[1] = q1
    esend2[1] = p1[end]
    coming += [send(esend2, erecv2, 1, 0), send(nsend2, nrecv2, 0, 1)]
    column, flux = complete(1, rx, ry, rz, p1, coming, nrecv2, erecv2, nrecv1, erecv1)

    def body(i, held):
        flux, h0, m1, m2 = held
        fx, fy, fz, flux = column(i, flux)
        vx[i], vy[i], vz[i] = fx, fy, fz
        m1 = m1 + fold(fx * rx[i] + fy * ry[i]) + fold(fz * rz[i])
        m2 = m2 + fold(fx * fx + fy * fy) + fold(fz * fz)
        return flux, pack_first(i, fy, h0), m1, m2

    flux, h0, m1, m2 = loop(body, (flux, zero, zero8, zero8))
    strip[2] = h0
    coming = [send(vx.at[0], vx.at[nx], -1, 0), send(strip.at[2], hy.at[2], 0, -1)]
    for copy in coming:
        copy.wait_recv()

    north_strip = hy[2]

    def body(i, m3):
        w, e, s = vx[i], vx[i + 1], vy[i]
        bottom, top = vz[i, pl.ds(0, levels), :], vz[i, pl.ds(1, levels), :]
        a, b, c = ix[i], iy[i], iz[i]
        n = jnp.where(last, pltpu.roll(north_strip, ny - 1 - i, 1), pltpu.roll(s, ny - 1, 1))
        sumx, sumy, sumz = w + e, s + n, bottom + top
        total = 3.0 * (a * sumx + b * sumy + c * sumz)
        p = total * di[i]
        p2[i] = p
        energy = (
            a * (w * w + e * e + sumx * sumx)
            + b * (s * s + n * n + sumy * sumy)
            + c * (bottom * bottom + top * top + sumz * sumz)
            - p * total
        )
        return m3 + fold(energy)

    m3 = loop(body, zero8)

    row = lax.broadcasted_iota(jnp.int32, (8, ny), 0)
    mine = zero8
    for n, m in enumerate((m0, m1, m2, m3)):
        mine = jnp.where(row == n, jnp.sum(m, 0, keepdims=True), mine)
    mom[0] = mine
    coming = [send(mom.at[0], slots1.at[d], d, 0) for d in range(1, npx)]
    for d, copy in enumerate(coming):
        copy.wait_recv()
        mine = mine + slots1[d + 1]
    mom[1] = mine
    coming = [send(mom.at[1], slots2.at[d], 0, d) for d in range(1, npy)]
    for d, copy in enumerate(coming):
        copy.wait_recv()
        mine = mine + slots2[d + 1]
    mine = jnp.sum(mine, 1, keepdims=True)
    m0, m1, m2, m3 = mine[0:1], mine[1:2], mine[2:3], mine[3:4]
    a0 = m0 / m1
    new = a0 * a0 * m2 - m0
    grown = 1.0 + new / m0
    curve = a0 * (a0 * m3 - grown * m2)
    good = (new > 0.0) & (curve > 0.0)
    a1 = jnp.where(good, new / jnp.where(good, curve, 1.0), 0.0)
    c0 = a0 + a1 * grown
    c1 = -a0 * a1
    c0 = jnp.broadcast_to(c0, (1, ny))
    c1 = jnp.broadcast_to(c1, (1, ny))

    def body(i, carry):
        ox[i] = xs[i] + c0 * rx[i] + c1 * vx[i]
        oy[i] = ys[i] + c0 * ry[i] + c1 * vy[i]
        faces = pl.ds(0, levels + 1)
        oz[i] = zs[i] + c0 * rz[i, faces, :] + c1 * vz[i, faces, :]
        op[i] = p0[i] + c0 * p1[i] + c1 * p2[i]
        return carry

    loop(body, 0)
    for copy in sent:
        copy.wait_send()


def local(npx, npy, metric, helmholtz, forcing, orientation, start_x, start_y, start_z):
    nx, levels, ny = start_x.shape
    faces = levels + 8
    cells = pltpu.VMEM((nx, levels, ny), F32)
    padded = pltpu.VMEM((nx + 1, levels, ny), F32)
    vertical = pltpu.VMEM((nx, faces, ny), F32)

    def tiles(n):
        return pltpu.VMEM((n, levels, ny), F32)

    sends = 14 + (npx - 1) + (npy - 1)
    return pl.pallas_call(
        functools.partial(kernel, npx, npy),
        out_shape=[jax.ShapeDtypeStruct(a.shape, F32) for a in (start_x, start_y, start_z, start_x)],
        in_specs=[pl.BlockSpec(memory_space=pl.ANY)] * 7,
        out_specs=[pl.BlockSpec(memory_space=pltpu.VMEM)] * 4,
        scratch_shapes=[
            pltpu.VMEM(metric.shape, metric.dtype),
            pltpu.VMEM(helmholtz.shape, helmholtz.dtype),
            pltpu.VMEM(forcing.shape, forcing.dtype),
            pltpu.VMEM(orientation.shape, orientation.dtype),
            padded, cells, pltpu.VMEM(start_z.shape, F32),
            cells, cells, cells, cells, cells, cells, cells,
            padded, cells, vertical, padded, cells, vertical,
            tiles(3), tiles(4), tiles(5), tiles(2), tiles(2),
            tiles(3), tiles(2), tiles(2), tiles(4), tiles(5), tiles(2), tiles(2),
            pltpu.VMEM((2, 8, ny), F32),
            pltpu.VMEM((npx, 8, ny), F32),
            pltpu.VMEM((npy, 8, ny), F32),
            pltpu.SemaphoreType.DMA((7,)),
            pltpu.SemaphoreType.DMA((sends,)),
            pltpu.SemaphoreType.DMA((sends,)),
        ],
        compiler_params=pltpu.CompilerParams(
            collective_id=0, has_side_effects=True, vmem_limit_bytes=40 * 1024 * 1024
        ),
    )(metric, helmholtz, forcing, orientation, start_x, start_y, start_z)


def solution(mesh):
    return jax.shard_map(
        functools.partial(local, mesh.shape["px"], mesh.shape["py"]),
        mesh=mesh,
        in_specs=(
            P(None, "px", None, "py"),
            P("px", None, "py"),
            P("px", None, "py"),
            P("px", "py"),
            P("px", None, "py"),
            P("px", None, "py"),
            P("px", None, "py"),
        ),
        out_specs=(P("px", None, "py"),) * 4,
        check_vma=False,
    )
```

time: 219 us -> 44.2 us (0.20)
  waiting for transfers between devices: 86.8 us -> 0 us
  blocking collectives: 75.1 us -> 0 us
  Pallas kernels: 0 us -> 35.5 us
  starting transfers between devices: 19.5 us -> 0 us
  other arithmetic: 16.7 us -> 0 us
  between operations: 14.2 us -> 0.69 us
    ppermute x14 -> x0, waiting for transfers between devices: 86.8 us -> none  [shifted(): lax.ppermute(x, axis, [(i, (i + by) % devices) for i in range(devices)])]
    psum x2 -> x0, blocking collectives: 75.1 us -> none  [pair_sums(): return lax.psum((norm_part, curve_part), ('px', 'py'))]
    pallas_call x0 -> x1, Pallas kernels: none -> 35.5 us  [local(): pl.pallas_call(functools.partial(kernel, npx, npy), out_shape=[jax.ShapeD...]
    ppermute x14 -> x0, starting transfers between devices: 19.5 us -> none  [shifted(): lax.ppermute(x, axis, [(i, (i + by) % devices) for i in range(devices)])]
    reduce_sum x6 -> x0, other arithmetic: 8.19 us -> none  [the longest x3 3.62 us: owned_inner(): jnp.sum(first_vec[2] * second_vec[2])]
    sub x6 -> x0, other arithmetic: 4.32 us -> none  [the longest x3 2.68 us: element(): inverse_z * (2.0 * trace_bottom + trace_top) - weight_z * pressure]
    unnamed x50 -> x16, local copies, waits for them, and re-layouts: 2.42 us -> 6.72 us
    slice x22 -> x0, local copies, waits for them, and re-layouts: 3.36 us -> none  [the longest x5 1.19 us: neighbours(): east_side = jnp.concatenate([field_x[1:], from_east], 0)]
  transfers between devices with their start and end apart: 14 -> 0, of which waited for: 9 -> 0; matrix products, arithmetic and copies ran while one was open for 3% -> 0% of each run, Pallas kernels for 0% -> 0%
where the time goes in v1:
time: 44.2 us; the launch traced here: 44 us
  Pallas kernels  35.5 us (80%)
  local copies, waits for them, and re-layouts  7.8 us (18%)
  between operations  0.69 us (2%)
    pallas_call x1, Pallas kernels, local(): pl.pallas_call(functools.partial(kernel, npx, npy), out_shape=[jax.ShapeD...  35.5 us
    unnamed x16, local copies, waits for them, and re-layouts  6.72 us
    pallas_call x1, local copies, waits for them, and re-layouts, local(): pl.pallas_call(functools.partial(kernel, npx, npy), out_shape=[jax.ShapeD...  1.09 us

profile of v1, /device:TPU:0, one launch (start us, length us, event | category | flops | bytes accessed | tf_op | source)
XLA Modules:
  0.0 44.0 jit_solution(13141211737924794305)
XLA Ops:
  0.6 0.0 copy-start.5
  0.6 0.0 copy-start.3
  0.7 0.0 copy-start
  0.7 1.2 %copy.11.sz_h = f32[40,25,128]{2,1,0:T(8,128)S(1)} copy(f32[40,25,128]{2,0,1:T(8,128)} %param.13) | data formatting | bytes 1024000 | tf_op args[6]
  1.9 0.0 copy-done.5
  1.9 0.0 copy-done.3
  1.9 0.1 copy-done
  2.1 0.0 copy-start.1
  2.1 1.0 %copy-done.1 = f32[40,24,128]{2,1,0:T(8,128)S(1)} copy-done((f32[40,24,128]{2,1,0:T(8,128)S(1)}, f32[40,24,128]{2,1,0:T(8,128)}, u32[]{:S(2)}) %copy-start.1) | copy-done | bytes 491544
  3.1 0.0 copy-start.2
  3.1 1.0 %copy-done.2 = f32[40,24,128]{2,1,0:T(8,128)S(1)} copy-done((f32[40,24,128]{2,1,0:T(8,128)S(1)}, f32[40,24,128]{2,1,0:T(8,128)}, u32[]{:S(2)}) %copy-start.2) | copy-done | bytes 491544
  4.1 0.0 copy-start.4
  4.1 0.9 %copy-done.4 = bf16[40,24,128]{2,1,0:T(8,128)(2,1)S(1)} copy-done((bf16[40,24,128]{2,1,0:T(8,128)(2,1)S(1)}, bf16[40,24,128]{2,1,0:T(8,128)(2,1)}, u32[]{:S(2)}) %copy-start.4) | copy-done | bytes 245784
  5.1 35.5 %shard_map.102 = (f32[40,24,128]{2,1,0:T(8,128)S(1)}, f32[40,24,128]{2,1,0:T(8,128)S(1)}, f32[40,25,128]{2,1,0:T(8,128)S(1)}, f32[40,24,128]{2,1,0:T(8,128)S(1)}) custom-call(bf16[3,40,24,128]{3,2,1,0:T(8,128)(2,1)S(1)} %copy-done, bf16[40,24,128]{2,1,0:T(8,128)(2,1)S(1)} %copy-done.3, bf16[40,24,128]{2,1,0:T(8,128)(2,1)S(1)} %copy-done.4, ...), custom_call_target="tpu_custom_call" | custom-call | tf_op jit(solution)/shard_map/pallas_call | solution.py:293
  40.6 1.1 %copy.12 = f32[40,25,128]{2,0,1:T(8,128)} copy(f32[40,25,128]{2,1,0:T(8,128)S(1)} %get-tuple-element.6) | data formatting | bytes 1024000 | tf_op jit(solution)/shard_map/pallas_call | solution.py:293
  41.6 0.8 %copy.16 = f32[40,24,128]{2,1,0:T(8,128)} copy(f32[40,24,128]{2,1,0:T(8,128)S(1)} %get-tuple-element.12) | data formatting | bytes 983040
  42.4 0.8 %copy.17 = f32[40,24,128]{2,1,0:T(8,128)} copy(f32[40,24,128]{2,1,0:T(8,128)S(1)} %get-tuple-element.13) | data formatting | bytes 983040
  43.2 0.8 %copy.18 = f32[40,24,128]{2,1,0:T(8,128)} copy(f32[40,24,128]{2,1,0:T(8,128)S(1)} %get-tuple-element.15) | data formatting | bytes 983040
Async XLA Ops:
  0.6 1.3 %copy-start.5 = (s32[40,128]{1,0:T(8,128)S(1)}, s32[40,128]{1,0:T(8,128)}, u32[]{:S(2)}) copy-start(s32[40,128]{1,0:T(8,128)} %ori_h.1) | copy-start | bytes 61444
  0.6 1.3 %copy-start.3 = (bf16[40,24,128]{2,1,0:T(8,128)(2,1)S(1)}, bf16[40,24,128]{2,1,0:T(8,128)(2,1)}, u32[]{:S(2)}) copy-start(bf16[40,24,128]{2,1,0:T(8,128)(2,1)} %hel_h.1) | copy-start | bytes 737284
  0.7 1.4 %copy-start = (bf16[3,40,24,128]{3,2,1,0:T(8,128)(2,1)S(1)}, bf16[3,40,24,128]{3,2,1,0:T(8,128)(2,1)}, u32[]{:S(2)}) copy-start(bf16[3,40,24,128]{3,2,1,0:T(8,128)(2,1)} %met_h.1) | copy-start | bytes 2211844
  2.1 1.0 %copy-start.1 = (f32[40,24,128]{2,1,0:T(8,128)S(1)}, f32[40,24,128]{2,1,0:T(8,128)}, u32[]{:S(2)}) copy-start(f32[40,24,128]{2,1,0:T(8,128)} %sx_h.1) | copy-start | bytes 1474564
  3.1 1.0 %copy-start.2 = (f32[40,24,128]{2,1,0:T(8,128)S(1)}, f32[40,24,128]{2,1,0:T(8,128)}, u32[]{:S(2)}) copy-start(f32[40,24,128]{2,1,0:T(8,128)} %sy_h.1) | copy-start | bytes 1474564
  4.1 0.9 %copy-start.4 = (bf16[40,24,128]{2,1,0:T(8,128)(2,1)S(1)}, bf16[40,24,128]{2,1,0:T(8,128)(2,1)}, u32[]{:S(2)}) copy-start(bf16[40,24,128]{2,1,0:T(8,128)(2,1)} %src_h.1) | copy-start | bytes 737284

commit v2 on v1

--- a/solution.py
+++ b/solution.py
@@ -9,6 +9,7 @@
 
 MESH = pl.DeviceIdType.MESH
 F32 = jnp.float32
+DIRECT = 64
 
 
 def fold(x):
@@ -27,10 +28,11 @@
     strip, nsend1, esend1, nsend2, esend2,
     hy, cx, cy, nrecv1, erecv1, nrecv2, erecv2,
     mom, slots1, slots2,
-    in_sem, send_sem, recv_sem,
+    in_sem, z_sem, out_sem, send_sem, recv_sem, all_sem,
 ):
     nx, levels, ny = hel.shape
-    unroll = next(u for u in (8, 5, 4, 2, 1) if nx % u == 0)
+    direct = npx * npy <= DIRECT
+    unroll = next(u for u in (10, 8, 5, 4, 2, 1) if nx % u == 0)
     px, py = lax.axis_index("px"), lax.axis_index("py")
 
     def device(dx, dy):
@@ -40,20 +42,25 @@
     for n, (a, b) in enumerate(
         (
             (sx_h, xs.at[pl.ds(0, nx)]), (sy_h, ys), (met_h, met), (ori_h, ori),
-            (hel_h, hel), (src_h, src), (sz_h, zs),
+            (hel_h, hel), (src_h, src),
         )
     ):
         copy = pltpu.make_async_copy(a, b, in_sem.at[n])
         copy.start()
         loads.append(copy)
+    for level in range(levels + 1):
+        copy = pltpu.make_async_copy(sz_h.at[level], zs.at[:, level, :], z_sem.at[level])
+        copy.start()
+        loads.append(copy)
 
     offsets = {(1, 0), (-1, 0), (0, 1), (0, -1), (-1, 1), (1, -1)}
     offsets |= {(d, 0) for d in range(1, npx)} | {(0, d) for d in range(1, npy)}
+    if direct:
+        offsets = {(a, b) for a in range(npx) for b in range(npy)}
     offsets = sorted({(a % npx, b % npy) for a, b in offsets} - {(0, 0)})
     barrier = pltpu.get_barrier_semaphore()
     for a, b in offsets:
         pl.semaphore_signal(barrier, inc=1, device_id=device(a, b), device_id_type=MESH)
-    pl.semaphore_wait(barrier, len(offsets))
 
     count = [0]
     sent = []
@@ -139,9 +146,7 @@
 
         return column, flux_west_halo
 
-    loads[0].wait()
-    coming = [send(xs.at[0], xs.at[nx], -1, 0), send(xs.at[0], cx.at[0], -1, 1)]
-    for copy in loads[1:]:
+    for copy in loads:
         copy.wait()
 
     def body(i, held):
@@ -169,8 +174,10 @@
     nsend1[3] = pack_last(nx, kx_end, k1)
     esend1[0], esend1[1], esend1[2] = xs[end], p0[end], ix[end]
     esend1[3], esend1[4] = kx_end, 3.0 * iy[end] * di[end]
-    coming += [
-        send(esend1, erecv1, 1, 0), send(nsend1, nrecv1, 0, 1),
+    pl.semaphore_wait(barrier, len(offsets))
+    coming = [
+        send(nsend1, nrecv1, 0, 1), send(esend1, erecv1, 1, 0),
+        send(xs.at[0], xs.at[nx], -1, 0), send(xs.at[0], cx.at[0], -1, 1),
         send(strip.at[0], hy.at[0], 0, -1), send(strip.at[0], cy.at[0], 1, -1),
     ]
 
@@ -215,16 +222,14 @@
     flux, h0, m1, m2 = loop(body, (flux, zero, zero8, zero8))
     strip[2] = h0
     coming = [send(vx.at[0], vx.at[nx], -1, 0), send(strip.at[2], hy.at[2], 0, -1)]
-    for copy in coming:
-        copy.wait_recv()
-
-    north_strip = hy[2]
-
-    def body(i, m3):
-        w, e, s = vx[i], vx[i + 1], vy[i]
+
+    def body(i, held):
+        s1, q1, m3 = held
+        w, s = vx[i], vy[i]
+        e = jnp.where(i < nx - 1, vx[jnp.minimum(i + 1, nx - 1)], 0.0)
         bottom, top = vz[i, pl.ds(0, levels), :], vz[i, pl.ds(1, levels), :]
         a, b, c = ix[i], iy[i], iz[i]
-        n = jnp.where(last, pltpu.roll(north_strip, ny - 1 - i, 1), pltpu.roll(s, ny - 1, 1))
+        n = jnp.where(last, 0.0, pltpu.roll(s, ny - 1, 1))
         sumx, sumy, sumz = w + e, s + n, bottom + top
         total = 3.0 * (a * sumx + b * sumy + c * sumz)
         p = total * di[i]
@@ -235,24 +240,49 @@
             + c * (bottom * bottom + top * top + sumz * sumz)
             - p * total
         )
-        return m3 + fold(energy)
-
-    m3 = loop(body, zero8)
+        return pack_last(i, s, s1), pack_last(i, p, q1), m3 + fold(energy)
+
+    s1, q1, m3 = loop(body, (zero, zero, zero8))
+    for copy in coming:
+        copy.wait_recv()
+    e = vx[nx]
+    grow = kx_end * e
+    m3 = m3 + fold(ix[end] * e * (2.0 * (e + vx[end]) - 6.0 * p2[end] - 3.0 * grow))
+    p2[end] = p2[end] + grow
+    n = hy[2]
+    q1 = q1 + jnp.where(lane == end, pltpu.roll(grow, nx, 1), 0.0)
+    grow = nsend1[3] * n
+    rest = nsend1[2] * n * (2.0 * (n + s1) - 6.0 * q1 - 3.0 * grow)
+    m3 = m3 + fold(jnp.where(lane < nx, rest, 0.0))
+    row_grow = jnp.where(lane < nx, grow, 0.0)
 
     row = lax.broadcasted_iota(jnp.int32, (8, ny), 0)
     mine = zero8
     for n, m in enumerate((m0, m1, m2, m3)):
         mine = jnp.where(row == n, jnp.sum(m, 0, keepdims=True), mine)
     mom[0] = mine
-    coming = [send(mom.at[0], slots1.at[d], d, 0) for d in range(1, npx)]
-    for d, copy in enumerate(coming):
-        copy.wait_recv()
-        mine = mine + slots1[d + 1]
-    mom[1] = mine
-    coming = [send(mom.at[1], slots2.at[d], 0, d) for d in range(1, npy)]
-    for d, copy in enumerate(coming):
-        copy.wait_recv()
-        mine = mine + slots2[d + 1]
+    if direct:
+        others = [(a, b) for a in range(npx) for b in range(npy)][1:]
+        for n, (a, b) in enumerate(others):
+            copy = pltpu.make_async_remote_copy(
+                src_ref=mom.at[0], dst_ref=slots1.at[n], send_sem=send_sem.at[14 + n],
+                recv_sem=all_sem, device_id=device(a, b), device_id_type=MESH,
+            )
+            copy.start()
+            sent.append(copy)
+        whole = slots1.at[pl.ds(0, len(others))]
+        pltpu.make_async_copy(whole, whole, all_sem).wait()
+        mine = mine + jnp.sum(slots1[: len(others)], 0)
+    else:
+        coming = [send(mom.at[0], slots1.at[d], d, 0) for d in range(1, npx)]
+        for d, copy in enumerate(coming):
+            copy.wait_recv()
+            mine = mine + slots1[d + 1]
+        mom[1] = mine
+        coming = [send(mom.at[1], slots2.at[d], 0, d) for d in range(1, npy)]
+        for d, copy in enumerate(coming):
+            copy.wait_recv()
+            mine = mine + slots2[d + 1]
     mine = jnp.sum(mine, 1, keepdims=True)
     m0, m1, m2, m3 = mine[0:1], mine[1:2], mine[2:3], mine[3:4]
     a0 = m0 / m1
@@ -266,15 +296,41 @@
     c0 = jnp.broadcast_to(c0, (1, ny))
     c1 = jnp.broadcast_to(c1, (1, ny))
 
+    stores = []
+
+    def store(n, source, target):
+        copy = pltpu.make_async_copy(source, target, out_sem.at[n])
+        copy.start()
+        stores.append(copy)
+
     def body(i, carry):
-        ox[i] = xs[i] + c0 * rx[i] + c1 * vx[i]
-        oy[i] = ys[i] + c0 * ry[i] + c1 * vy[i]
         faces = pl.ds(0, levels + 1)
-        oz[i] = zs[i] + c0 * rz[i, faces, :] + c1 * vz[i, faces, :]
-        op[i] = p0[i] + c0 * p1[i] + c1 * p2[i]
+        zs[i] = zs[i] + c0 * rz[i, faces, :] + c1 * vz[i, faces, :]
         return carry
 
     loop(body, 0)
+    for level in range(levels + 1):
+        store(3 + level, zs.at[:, level, :], oz.at[level])
+    for n, (made, base, once, twice, target) in enumerate(
+        ((ix, xs, rx, vx, ox), (iy, ys, ry, vy, oy))
+    ):
+
+        def body(i, carry):
+            made[i] = base[i] + c0 * once[i] + c1 * twice[i]
+            return carry
+
+        loop(body, 0)
+        store(n, made, target)
+
+    def body(i, carry):
+        halo = pltpu.roll(row_grow, ny - 1 - i, 1)
+        iz[i] = p0[i] + c0 * p1[i] + c1 * (p2[i] + jnp.where(last, halo, 0.0))
+        return carry
+
+    loop(body, 0)
+    store(2, iz, op)
+    for copy in stores:
+        copy.wait()
     for copy in sent:
         copy.wait_send()
 
@@ -289,33 +345,39 @@
     def tiles(n):
         return pltpu.VMEM((n, levels, ny), F32)
 
-    sends = 14 + (npx - 1) + (npy - 1)
-    return pl.pallas_call(
+    direct = npx * npy <= DIRECT
+    sends = 14 + (npx * npy - 1 if direct else npx + npy - 2)
+    start_z = jnp.swapaxes(start_z, 0, 1)
+    x, y, z, pressure = pl.pallas_call(
         functools.partial(kernel, npx, npy),
         out_shape=[jax.ShapeDtypeStruct(a.shape, F32) for a in (start_x, start_y, start_z, start_x)],
-        in_specs=[pl.BlockSpec(memory_space=pl.ANY)] * 7,
-        out_specs=[pl.BlockSpec(memory_space=pltpu.VMEM)] * 4,
+        in_specs=[pl.BlockSpec(memory_space=pltpu.HBM)] * 7,
+        out_specs=[pl.BlockSpec(memory_space=pl.ANY)] * 4,
         scratch_shapes=[
             pltpu.VMEM(metric.shape, metric.dtype),
             pltpu.VMEM(helmholtz.shape, helmholtz.dtype),
             pltpu.VMEM(forcing.shape, forcing.dtype),
             pltpu.VMEM(orientation.shape, orientation.dtype),
-            padded, cells, pltpu.VMEM(start_z.shape, F32),
+            padded, cells, pltpu.VMEM((nx, levels + 1, ny), F32),
             cells, cells, cells, cells, cells, cells, cells,
             padded, cells, vertical, padded, cells, vertical,
             tiles(3), tiles(4), tiles(5), tiles(2), tiles(2),
             tiles(3), tiles(2), tiles(2), tiles(4), tiles(5), tiles(2), tiles(2),
             pltpu.VMEM((2, 8, ny), F32),
-            pltpu.VMEM((npx, 8, ny), F32),
+            pltpu.VMEM((npx * npy if direct else npx, 8, ny), F32),
             pltpu.VMEM((npy, 8, ny), F32),
-            pltpu.SemaphoreType.DMA((7,)),
+            pltpu.SemaphoreType.DMA((6,)),
+            pltpu.SemaphoreType.DMA((levels + 1,)),
+            pltpu.SemaphoreType.DMA((levels + 4,)),
             pltpu.SemaphoreType.DMA((sends,)),
             pltpu.SemaphoreType.DMA((sends,)),
+            pltpu.SemaphoreType.DMA,
         ],
         compiler_params=pltpu.CompilerParams(
             collective_id=0, has_side_effects=True, vmem_limit_bytes=40 * 1024 * 1024
         ),
-    )(metric, helmholtz, forcing, orientation, start_x, start_y, start_z)
+    )(*[pltpu.with_memory_space_constraint(a, pltpu.HBM) for a in (metric, helmholtz, forcing, orientation, start_x, start_y, start_z)])
+    return x, y, jnp.swapaxes(z, 0, 1), pressure
 
 
 def solution(mesh):

time: 44.2 us -> 36.6 us (0.83)
  local copies, waits for them, and re-layouts: 7.8 us -> 3.12 us
  Pallas kernels: 35.5 us -> 32.6 us
    unnamed x16 -> x4, local copies, waits for them, and re-layouts: 6.72 us -> 3.12 us
    pallas_call x1, Pallas kernels: 35.5 us -> 32.6 us  [local(): pl.pallas_call(functools.partial(kernel, npx, npy), out_shape=[jax.ShapeD...]
    pallas_call x1 -> x0, local copies, waits for them, and re-layouts: 1.09 us -> none  [local(): pl.pallas_call(functools.partial(kernel, npx, npy), out_shape=[jax.ShapeD...]
where the time goes in v2:
time: 36.6 us; the launch traced here: 36.4 us
  Pallas kernels  32.6 us (89%)
  local copies, waits for them, and re-layouts  3.12 us (9%)
  between operations  0.64 us (2%)
    pallas_call x1, Pallas kernels, local(): pl.pallas_call(functools.partial(kernel, npx, npy), out_shape=[jax.ShapeD...  32.6 us
    unnamed x4, local copies, waits for them, and re-layouts  3.12 us

profile of v2, /device:TPU:0, one launch (start us, length us, event | category | flops | bytes accessed | tf_op | source)
XLA Modules:
  0.0 36.4 jit_solution(18150203740207000872)
XLA Ops:
  0.6 32.6 %shard_map.102 = (f32[40,24,128]{2,1,0:T(8,128)S(1)}, f32[40,24,128]{2,1,0:T(8,128)S(1)}, f32[25,40,128]{2,1,0:T(8,128)S(1)}, f32[40,24,128]{2,1,0:T(8,128)S(1)}) custom-call(bf16[3,40,24,128]{3,2,1,0:T(8,128)(2,1)} %met_h.1, bf16[40,24,128]{2,1,0:T(8,128)(2,1)} %hel_h.1, bf16[40,24,128]{2,1,0:T(8,128)(2,1)} %src_h.1, s32[40,128]{1,0:T(8,128)} %ori_h.1, ...), custom_call_target="tpu_custom_call" | custom-call | tf_op jit(solution)/shard_map/pallas_call | solution.py:351
  33.3 0.8 %copy.15 = f32[40,24,128]{2,1,0:T(8,128)} copy(f32[40,24,128]{2,1,0:T(8,128)S(1)} %get-tuple-element.16) | data formatting | bytes 983040
  34.1 0.8 %copy.16 = f32[40,24,128]{2,1,0:T(8,128)} copy(f32[40,24,128]{2,1,0:T(8,128)S(1)} %get-tuple-element.17) | data formatting | bytes 983040
  34.8 0.8 %copy.17 = f32[40,25,128]{2,0,1:T(8,128)} copy(f32[40,25,128]{2,0,1:T(8,128)S(1)} %bitcast.2) | data formatting | bytes 1024000
  35.6 0.8 %copy.18 = f32[40,24,128]{2,1,0:T(8,128)} copy(f32[40,24,128]{2,1,0:T(8,128)S(1)} %get-tuple-element.19) | data formatting | bytes 983040
